TPU v7x, 32 devices: a 4x2x2 block of a 4x4x8 slice. The times are simulated.
32 devices in a mesh: replica: 4 (over y, z), ep: 8 (over x, core).
Axes of the slice: x: 4, y: 2, z: 2, core: 2. Of those that a mesh axis runs over, the one named last changes fastest.
The devices are a block of a 4x4x8 slice.
Arguments:
- tok_in: bfloat16 [8192, 1024], P(('replica', 'ep')), parts along dimension 0
- routes: int32 [2, 8192, 8], P(None, ('replica', 'ep')), parts along dimension 1
- gate_vals: float32 [2, 8192, 8], P(None, ('replica', 'ep')), parts along dimension 1
- w_gate: bfloat16 [2, 64, 1024, 512], P(None, ('replica', 'ep')), parts along dimension 1
- w_up: bfloat16 [2, 64, 1024, 512], P(None, ('replica', 'ep')), parts along dimension 1
- w_down: bfloat16 [2, 64, 512, 1024], P(None, ('replica', 'ep')), parts along dimension 1
- sh_gate: bfloat16 [2, 1024, 512], replicated
- sh_up: bfloat16 [2, 1024, 512], replicated
- sh_down: bfloat16 [2, 512, 1024], replicated
- old_map: int32 [2, 64], P(None, 'replica'), parts along dimension 1
- move_slot: int32 [2, 8], P(None, 'replica'), parts along dimension 1
- move_expert: int32 [2, 8], P(None, 'replica'), parts along dimension 1
Outputs:
- output 1: bfloat16 [8192, 1024], P(('replica', 'ep')), parts along dimension 0
- output 2: bfloat16 [2, 64, 1024, 512], P(None, ('replica', 'ep')), parts along dimension 1
- output 3: bfloat16 [2, 64, 1024, 512], P(None, ('replica', 'ep')), parts along dimension 1
- output 4: bfloat16 [2, 64, 512, 1024], P(None, ('replica', 'ep')), parts along dimension 1
There are 4 independent parts. A program takes and returns all parts, laid end to end along the dimension named above; an argument that names none is the same for every part.
All inputs are finite; a program needn't handle non-finite values.
Results may differ from a plain program's by a relative error of at most 0.0115662.
Values are sent between devices in bfloat16 or wider.
A program may use at most 768 MiB of HBM per device.

v0:
```python
import jax
import jax.numpy as jnp
from jax import lax
from jax.sharding import PartitionSpec as P

TOKEN_AXES = ('replica', 'ep')


def first_holder(slot_map, wanted):
    slot_ids = jnp.arange(slot_map.shape[0], dtype=jnp.int32)
    hit_mask = slot_map[None, :] == wanted[:, None]
    return jnp.min(jnp.where(hit_mask, slot_ids[None, :], slot_map.shape[0]), axis=1)


def swiglu(hidden, w_gate, w_up, w_down):
    gate_proj = jnp.dot(hidden, w_gate, preferred_element_type=jnp.float32)
    up_proj = jnp.dot(hidden, w_up, preferred_element_type=jnp.float32)
    inner_act = (jax.nn.silu(gate_proj) * up_proj).astype(jnp.bfloat16)
    return jnp.dot(inner_act, w_down, preferred_element_type=jnp.float32)


def send_moved(weights, slot_map, move_expert, slots_dev, my_dev):
    source = first_holder(slot_map, move_expert)
    is_source = (source // slots_dev) == my_dev
    local_idx = source % slots_dev
    return tuple(jnp.where(is_source[:, None, None], jnp.take(weight_arr, local_idx, axis=0), jnp.zeros((), weight_arr.dtype)) for weight_arr in weights)


def place_moved(weights, arrived, move_slot, slots_dev, my_dev):
    local_ids = my_dev * slots_dev + jnp.arange(slots_dev, dtype=jnp.int32)
    match_mask = (move_slot[None, :] == local_ids[:, None]).astype(jnp.int32)
    is_target = jnp.max(match_mask, axis=1) > 0
    pick_idx = jnp.argmax(match_mask, axis=1)
    return tuple(jnp.where(is_target[:, None, None], jnp.take(arrived_arr, pick_idx, axis=0), weight_arr) for arrived_arr, weight_arr in zip(arrived, weights))


def moe_layer(hidden, route_all, gate_all, expert_w, shared_w, slot_map, slots_dev, my_dev):
    gathered = lax.all_gather(hidden, 'ep', axis=0, tiled=True)
    slot_ids = jnp.arange(slot_map.shape[0], dtype=jnp.int32)
    serve_all = (first_holder(slot_map, slot_map) == slot_ids).astype(jnp.float32)
    local_map = lax.dynamic_slice_in_dim(slot_map, my_dev * slots_dev, slots_dev)
    local_serve = lax.dynamic_slice_in_dim(serve_all, my_dev * slots_dev, slots_dev)
    hit_mask = route_all[:, :, None] == local_map[None, None, :]
    gate_coef = jnp.sum(jnp.where(hit_mask, gate_all[:, :, None], 0.0), axis=1) * local_serve[None, :]
    gate_proj = jnp.einsum('nd,jdf->jnf', gathered, expert_w[0], preferred_element_type=jnp.float32)
    up_proj = jnp.einsum('nd,jdf->jnf', gathered, expert_w[1], preferred_element_type=jnp.float32)
    inner_act = (jax.nn.silu(gate_proj) * up_proj).astype(jnp.bfloat16)
    expert_out = jnp.einsum('jnf,jfd->jnd', inner_act, expert_w[2], preferred_element_type=jnp.float32)
    partial_sum = jnp.sum(expert_out * gate_coef.T[:, :, None], axis=0)
    combined = lax.psum_scatter(partial_sum, 'ep', scatter_dimension=0, tiled=True)
    shared_out = swiglu(hidden, shared_w[0], shared_w[1], shared_w[2])
    return (hidden.astype(jnp.float32) + shared_out + combined).astype(jnp.bfloat16)


def solution(mesh):
    def body(tok_in, routes, gate_vals, w_gate, w_up, w_down, sh_gate, sh_up, sh_down, old_map, move_slot, move_expert):
        my_dev = lax.axis_index('ep')
        slots_dev = w_gate.shape[1]
        route_all = lax.all_gather(routes, 'ep', axis=1, tiled=True)
        gate_all = lax.all_gather(gate_vals, 'ep', axis=1, tiled=True)
        hidden = tok_in
        placed = []
        for layer_idx in range(2):
            layer_w = (w_gate[layer_idx], w_up[layer_idx], w_down[layer_idx])
            outgoing = send_moved(layer_w, old_map[layer_idx], move_expert[layer_idx], slots_dev, my_dev)
            arrived = lax.psum(outgoing, 'ep')
            new_w = place_moved(layer_w, arrived, move_slot[layer_idx], slots_dev, my_dev)
            new_map = old_map[layer_idx].at[move_slot[layer_idx]].set(move_expert[layer_idx])
            shared_w = (sh_gate[layer_idx], sh_up[layer_idx], sh_down[layer_idx])
            hidden = moe_layer(hidden, route_all[layer_idx], gate_all[layer_idx], new_w, shared_w, new_map, slots_dev, my_dev)
            placed.append(new_w)
        new_gate = jnp.stack([placed[0][0], placed[1][0]])
        new_up = jnp.stack([placed[0][1], placed[1][1]])
        new_down = jnp.stack([placed[0][2], placed[1][2]])
        return (hidden, new_gate, new_up, new_down)

    weight_spec = P(None, TOKEN_AXES, None, None)
    route_spec = P(None, TOKEN_AXES, None)
    map_spec = P(None, 'replica')
    shared_spec = P(None, None, None)
    tok_spec = P(TOKEN_AXES, None)
    return jax.shard_map(body, mesh=mesh, in_specs=(tok_spec, route_spec, route_spec, weight_spec, weight_spec, weight_spec, shared_spec, shared_spec, shared_spec, map_spec, map_spec, map_spec), out_specs=(tok_spec, weight_spec, weight_spec, weight_spec), check_vma=False)
```

profile of v0, /device:TPU:81, one launch (start us, length us, event | category | flops | bytes accessed | tf_op | source)
XLA Modules:
  0.0 428.3 jit_solution(6976679255225075448)
XLA Ops:
  7.2 0.8 slice_bitcast_fusion.13
  8.0 0.8 slice_bitcast_fusion.12
  8.8 4.7 %slice_bitcast_fusion.1 = (bf16[2,1024,512]{2,1,0:T(8,128)(2,1)}, bf16[2,1024,512]{2,1,0:T(8,128)(2,1)}) fusion(bf16[2,2,1024,512]{3,2,1,0:T(8,128)(2,1)} %param.20), kind=kLoop, calls=%fused_computation.52 | loop fusion | bytes 8388608 | tf_op jit(solution)/shard_map/squeeze | solution.py:64
  13.4 0.2 fusion.58
  13.7 2.3 slice_bitcast_fusion.2
  16.0 2.3 gather_fusion.2
  18.3 3.6 gather_fusion
  21.9 4.6 %slice_bitcast_fusion = (bf16[2,512,1024]{2,1,0:T(8,128)(2,1)}, bf16[2,512,1024]{2,1,0:T(8,128)(2,1)}) fusion(bf16[2,2,512,1024]{3,2,1,0:T(8,128)(2,1)} %param.21), kind=kLoop, calls=%fused_computation.51 | loop fusion | bytes 8388608 | tf_op jit(solution)/shard_map/squeeze | solution.py:64
  26.5 3.6 gather_fusion.4
  30.1 3.6 gather_fusion.8
  33.7 3.6 gather_fusion.6
  37.3 3.7 gather_fusion.10
  40.9 3.4 select_select_fusion.7
  44.3 2.5 select_select_fusion.9
  46.8 1.6 select_select_fusion.1
  48.5 0.7 copy-done.3
  49.2 0.6 copy-done.4
  49.8 2.5 select_select_fusion.3
  52.4 0.7 all-gather.3.cloned.1.call-update
  53.3 0.6 scatter_fusion
  53.9 0.1 dynamic_slice.12
  54.0 0.2 select_reduce_fusion.3
  54.1 0.1 dynamic_slice.13
  54.2 14.9 %all_gather.14 = f32[2,2048,8]{1,2,0:T(8,128)S(1)} all-gather(f32[2,256,8]{1,2,0:T(8,128)S(1)} %copy-done.10), channel_id=1, replica_groups=mesh['replica'=4,'ep'=8] {'ep'}, dimensions={1}, use_global_device_ids=true | all-gather | bytes 147456 | tf_op jit(solution)/shard_map/all_gather | solution.py:60
  69.1 13.0 %all_gather.13 = s32[2,2048,8]{1,2,0:T(8,128)S(1)} all-gather(s32[2,256,8]{1,2,0:T(8,128)S(1)} %copy-done.11), channel_id=1, replica_groups=mesh['replica'=4,'ep'=8] {'ep'}, dimensions={1}, use_global_device_ids=true | all-gather | bytes 147456 | tf_op jit(solution)/shard_map/all_gather | solution.py:59
  82.1 0.9 fusion.54
  83.0 0.2 fusion.57
  83.3 0.1 select_reduce_fusion.1
  83.4 0.1 multiply_bitcast_fusion.1
  83.5 111.3 %all-reduce.3.cloned.1.call-done = (bf16[2,1024,512]{2,1,0:T(8,128)(2,1)}, bf16[2,1024,512]{2,1,0:T(8,128)(2,1)}, bf16[2,512,1024]{2,1,0:T(8,128)(2,1)}, bf16[2,...) async-done(((bf16[2,1024,512]{2,1,0:T(8,128)(2,1)}, bf16[2,1024,512]{2,1,0:T(8,128)(2,1)}, bf16[2,512,1024]{2,1,0:T(8,128)(2,1)}, ...) | async-done | bytes 12582928 | tf_op jit(solution)/shard_map/psum | solution.py:66
  194.8 2.3 gather_fusion.1
  197.1 3.6 gather_fusion.3
  200.7 3.6 gather_fusion.5
  204.2 21.5 %all-gather.3.cloned.1.call-done = bf16[2048,1024]{1,0:T(8,128)(2,1)} async-done(((bf16[256,1024]{1,0:T(8,128)(2,1)}), bf16[2048,1024]{1,0:T(8,128)(2,1)}) %all-gather.3.cloned.1.call-update) | async-done | bytes 4194320 | tf_op jit(solution)/shard_map/all_gather | solution.py:38
  225.7 10.8 %fusion.12 = f32[2,512,2048]{2,1,0:T(8,128)} fusion(bf16[2048,1024]{1,0:T(8,128)(2,1)} %all-gather.3.cloned.1.call-done, bf16[2,1024,512]{2,1,0:T(8,128)(2,1)S(1)} %gather_fusion.1, pred[2]{0:T(512)(128)(4,1)S(1)} %get-tuple-element.56, pred[2]{0:T(512)(128)(4,1)S(1)} %get-tuple-element.57, bf16[2,2,1024,512]{3,2,1,0:T(8,128)(2,1)} %param.19), kind=kOutput, calls=%fused_computation.37 | convolution fusion | flops 4297064448 | bytes 16777220 | tf_op jit(solution)/shard_map/nd,jdf->jnf/dot_general | solution.py:45
  236.5 20.2 %multiply_reduce_fusion.1 = f32[2048,1024]{1,0:T(8,128)} fusion(f32[2,2048]{1,0:T(2,128)S(1)} %multiply_bitcast_fusion.1, f32[2,512,2048]{2,1,0:T(8,128)} %fusion.12, bf16[2048,1024]{1,0:T(8,128)(2,1)} %all-gather.3.cloned.1.call-done, bf16[2,1024,512]{2,1,0:T(8,128)(2,1)} %gather_fusion.3, pred[2]{0:T(512)(128)(4,1)S(1)} %get-tuple-element.56, ...), kind=kOutput, calls=%fused_computation.15 | convolution fusion | flops 8613003264 | bytes 29378560 | tf_op jit(solution)/shard_map/jnf,jfd->jnd/dot_general | solution.py:48
  256.8 0.9 copy-done.8
  257.7 1.7 fusion.32
  259.4 46.0 %reduce-scatter.3.cloned.1.call-done = f32[256,1024]{1,0:T(8,128)} async-done(((f32[2048,1024]{1,0:T(8,128)}), f32[256,1024]{1,0:T(8,128)}) %reduce-scatter.3.cloned.1.call-update) | async-done | bytes 1048592 | tf_op jit(solution)/shard_map/reduce_scatter | solution.py:50
  305.4 3.5 fusion.20
  309.0 0.6 scatter_fusion.1
  309.6 0.1 dynamic_slice.14
  309.6 0.2 select_reduce_fusion.2
  309.8 0.1 dynamic_slice.15
  309.9 0.9 fusion.56
  310.8 0.1 select_reduce_fusion
  311.0 3.6 gather_fusion.7
  314.6 3.6 gather_fusion.9
  318.2 3.6 gather_fusion.11
  321.8 16.5 %all-gather.5.cloned.1.call-done = bf16[2048,1024]{1,0:T(8,128)(2,1)} async-done(((bf16[256,1024]{1,0:T(8,128)(2,1)}), bf16[2048,1024]{1,0:T(8,128)(2,1)}) %all-gather.5.cloned.1.call-update) | async-done | bytes 4194320 | tf_op jit(solution)/shard_map/all_gather | solution.py:38
  338.3 11.3 %fusion.9 = f32[2,512,2048]{2,1,0:T(8,128)} fusion(bf16[2048,1024]{1,0:T(8,128)(2,1)} %all-gather.5.cloned.1.call-done, bf16[2,1024,512]{2,1,0:T(8,128)(2,1)} %gather_fusion.7, pred[2]{0:T(512)(128)(4,1)S(1)} %get-tuple-element.58, pred[2]{0:T(512)(128)(4,1)S(1)} %get-tuple-element.59, bf16[2,2,1024,512]{3,2,1,0:T(8,128)(2,1)} %param.19), kind=kOutput, calls=%fused_computation.34 | convolution fusion | flops 4297064448 | bytes 16777220 | tf_op jit(solution)/shard_map/nd,jdf->jnf/dot_general | solution.py:45
  349.6 20.2 %multiply_reduce_fusion = f32[2048,1024]{1,0:T(8,128)} fusion(f32[2,2048]{1,0:T(2,128)S(1)} %multiply_bitcast_fusion, f32[2,512,2048]{2,1,0:T(8,128)} %fusion.9, bf16[2048,1024]{1,0:T(8,128)(2,1)} %all-gather.5.cloned.1.call-done, bf16[2,1024,512]{2,1,0:T(8,128)(2,1)} %gather_fusion.9, pred[2]{0:T(512)(128)(4,1)S(1)} %get-tuple-element.58, ...), kind=kOutput, calls=%fused_computation.14 | convolution fusion | flops 8613003264 | bytes 29378560 | tf_op jit(solution)/shard_map/jnf,jfd->jnd/dot_general | solution.py:48
  369.9 6.1 %fusion.68 = (bf16[1,2,1024,512]{3,2,1,0:T(8,128)(2,1)S(1)}, bf16[1,2,1024,512]{3,2,1,0:T(8,128)(2,1)S(1)}, bf16[1,2,1024,512]{3,2,1,0:T(8,128)(2,1)S(1)}, bf16[1,2,1024,512]{3,2,1,0:T(8,128)(2,1)S(1)}) fusion(bf16[2,2,1024,512]{3,2,1,0:T(8,128)(2,1)} %param.19, bf16[2,1024,512]{2,1,0:T(8,128)(2,1)S(1)} %gather_fusion.1, ...), kind=kLoop, calls=%fused_computation.156 | loop fusion | flops 8388608 | bytes 25165832 | tf_op jit(solution)/shard_map/stack | solution.py:72
  376.1 2.4 pad_maximum_fusion
  378.4 2.5 pad_maximum_fusion.1
  380.9 1.2 copy-done.1
  382.1 0.7 copy-done.6
  382.8 0.6 copy-done.7
  383.4 0.5 fusion.70
  384.0 2.4 pad_maximum_fusion.2
  386.4 0.3 copy-done.13
  386.7 0.4 fusion.27
  387.1 31.4 %reduce-scatter.5.cloned.1.call-done = f32[256,1024]{1,0:T(8,128)} async-done(((f32[2048,1024]{1,0:T(8,128)}), f32[256,1024]{1,0:T(8,128)}) %reduce-scatter.5.cloned.1.call-update) | async-done | bytes 1048592 | tf_op jit(solution)/shard_map/reduce_scatter | solution.py:50
  418.5 3.2 fusion.21
  (50 shorter events, 0.8 us)
Async XLA Ops:
  7.2 187.6 %all-reduce.3.cloned.1.call-start = ((), (), s32[]{:S(2)}) async-start(), calls=%async_computation.6 | async-start | bytes 25165824 | tf_op jit(solution)/shard_map/psum | solution.py:66
  8.8 4.9 %copy-start = (bf16[2,2,1024,512]{3,2,1,0:T(8,128)(2,1)S(1)}, bf16[2,2,1024,512]{3,2,1,0:T(8,128)(2,1)}, u32[]{:S(2)}) copy-start(bf16[2,2,1024,512]{3,2,1,0:T(8,128)(2,1)} %param.19) | copy-start | bytes 12582916
  40.9 3.4 copy-start.2
  44.3 2.5 copy-start.5
  46.8 2.3 copy-start.3
  46.8 3.0 copy-start.4
  52.3 1.0 copy-start.12
  52.3 1.9 copy-start.10
  52.3 16.8 %copy-start.11 = (s32[2,256,8]{1,2,0:T(8,128)S(1)}, s32[2,256,8]{1,2,0:T(8,128)}, u32[]{:S(2)}) copy-start(s32[2,256,8]{1,2,0:T(8,128)} %param.17) | copy-start | bytes 49156
  52.4 173.3 %all-gather.3.cloned.1.call-start = ((), (), s32[]{:S(2)}) async-start(), calls=%async_computation.2 | async-start | bytes 4718592 | tf_op jit(solution)/shard_map/all_gather | solution.py:38
  53.2 252.2 %reduce-scatter.3.cloned.1.call-start = ((), (), s32[]{:S(2)}) async-start(), calls=%async_computation.3 | async-start | bytes 9437184 | tf_op jit(solution)/shard_map/reduce_scatter | solution.py:50
  256.7 1.0 copy-start.8
  256.8 81.5 %all-gather.5.cloned.1.call-start = ((), (), s32[]{:S(2)}) async-start(), calls=%async_computation.4 | async-start | bytes 4718592 | tf_op jit(solution)/shard_map/all_gather | solution.py:38
  308.9 109.6 %reduce-scatter.5.cloned.1.call-start = ((), (), s32[]{:S(2)}) async-start(), calls=%async_computation.5 | async-start | bytes 9437184 | tf_op jit(solution)/shard_map/reduce_scatter | solution.py:50
  378.4 3.7 copy-start.1
  378.4 4.4 %copy-start.6 = (bf16[2,512,1024]{2,1,0:T(8,128)(2,1)S(1)}, bf16[2,512,1024]{2,1,0:T(8,128)(2,1)}, u32[]{:S(2)}) copy-start(bf16[2,512,1024]{2,1,0:T(8,128)(2,1)} %gather_fusion.5) | copy-start | bytes 6291460
  378.4 5.0 %copy-start.7 = (bf16[2,512,1024]{2,1,0:T(8,128)(2,1)S(1)}, bf16[2,512,1024]{2,1,0:T(8,128)(2,1)}, u32[]{:S(2)}) copy-start(bf16[2,512,1024]{2,1,0:T(8,128)(2,1)} %gather_fusion.11) | copy-start | bytes 6291460
  383.9 2.4 copy-start.9
  384.0 2.7 copy-start.13
  386.7 31.8 %copy-start.14 = (bf16[2,512,1024]{2,1,0:T(8,128)(2,1)S(1)}, bf16[2,512,1024]{2,1,0:T(8,128)(2,1)}, u32[]{:S(2)}) copy-start(bf16[2,512,1024]{2,1,0:T(8,128)(2,1)} %param.24) | copy-start | bytes 6291460
Sparse Core Ops, SparseCore 0:
  52.5 142.2 all-reduce.2
  196.4 29.2 all-gather.2
  256.9 48.4 reduce-scatter.2
  309.0 29.2 all-gather.4
  370.0 48.4 reduce-scatter.4
where the time goes:
time: 429 us; the launch traced here: 428 us
  waiting for transfers between devices  228 us (53%)
  matrix products  71.3 us (17%)
  local copies, waits for them, and re-layouts  60.2 us (14%)
  blocking collectives  27.9 us (7%)
  other arithmetic  26.9 us (6%)
  between operations  14 us (3%)
    psum x1, waiting for transfers between devices, body(): arrived = lax.psum(outgoing, 'ep')  111 us
    reduce_scatter x2, waiting for transfers between devices, moe_layer(): lax.psum_scatter(partial_sum, 'ep', scatter_dimension=0, tiled=True)  77.4 us
    dot_general x2, matrix products, moe_layer(): jnp.einsum('jnf,jfd->jnd', inner_act, expert_w[2], preferred_element_type...  40.5 us
    all_gather x2, waiting for transfers between devices, moe_layer(): gathered = lax.all_gather(hidden, 'ep', axis=0, tiled=True)  38 us
    dot_general x2, matrix products, moe_layer(): jnp.einsum('nd,jdf->jnf', gathered, expert_w[0], preferred_element_type=j...  22.1 us
    gather x6, local copies, waits for them, and re-layouts, send_moved(): jnp.take(weight_arr, local_idx, axis=0)  20.3 us
    gather x6, local copies, waits for them, and re-layouts, place_moved(): jnp.take(arrived_arr, pick_idx, axis=0)  20.2 us
    all_gather x1, blocking collectives, body(): gate_all = lax.all_gather(gate_vals, 'ep', axis=1, tiled=True)  14.9 us
  transfers between devices with their start and end apart: 5, of which 5 were waited for; matrix products, arithmetic and copies ran while one was open for 9% of the time, Pallas kernels for 0%

commit v1 on v0

v1 whole, which is shorter than its diff:
```python
import functools

import jax
import jax.numpy as jnp
from jax import lax
from jax.experimental import pallas as pl
from jax.experimental.pallas import tpu as pltpu
from jax.sharding import PartitionSpec as P

TOKEN_AXES = ('replica', 'ep')
MESH = pl.DeviceIdType.MESH
CHUNKS = 4
PIECE = 16
LAG = 2
SEND_SLOTS = 4
OUT_SLOTS = 4
RECV_SEMS = 8
RECV_SLOTS = 16
LAYERS = 2
PLACE = {'u1': (2, 2), 'u2': (2, 2), 'u3': (2, 2), 'own': (2, 2), 'sum': (1, 1), 'fin': (1, 1)}


def kernel(n_chip, dims, tab, coef, tok, wg, wu, wd, sg, su, sd,
           tok_out, w_out,
           wall, shw, tbuf, pbuf, rpure, ropp, rsum, crecv, mrecv, msend, mout,
           own_sem, w_send, w_recv, sh_sem, tok_sem, c_send, c_recv,
           ag_send, ag_recv, rl_send, rl_recv, pu_send, pu_recv,
           op_send, op_recv, sm_send, sm_recv,
           mv_send, mv_recv, mo_local, mo_send, mo_recv):
    toks, d_model, d_ff = dims
    half = toks // 2
    ch = half // CHUNKS
    quarter = d_model // 4
    per_phase = quarter // PIECE
    n_piece = 3 * per_phase
    n_step = n_piece + 2 * LAG
    f32, bf16 = jnp.float32, jnp.bfloat16

    me = lax.axis_index('ep')
    chip = me // 2
    core = lax.rem(me, 2)
    dev_r = lax.rem(chip + 1, n_chip) * 2 + core
    dev_l = lax.rem(chip + n_chip - 1, n_chip) * 2 + core
    dev_o = lax.rem(chip + 2, n_chip) * 2 + core
    dev_p = chip * 2 + 1 - core

    def rdma(src, dst, ss, rs, dev):
        return pltpu.make_async_remote_copy(src_ref=src, dst_ref=dst, send_sem=ss, recv_sem=rs,
                                            device_id={'ep': dev}, device_id_type=MESH)

    base = core * 2
    mine = pl.ds(base, 2)
    loads = []

    def weight_parts(l, g, u, d):
        return [(g, pl.ds(0, d_model), None), (u, pl.ds(d_model, d_model), None),
                (d, pl.ds(2 * d_model, d_ff), 0), (d, pl.ds(2 * d_model + d_ff, d_ff), 1)]

    def src_of(ref, col, l):
        if col is None:
            return ref.at[l]
        cols = pl.ds(col * d_ff, d_ff)
        return ref.at[l, :, :, cols] if len(ref.shape) == 4 else ref.at[l, :, cols]

    def own_load(l):
        return [pltpu.make_async_copy(src_of(r, c, l), wall.at[l, mine, rows, :], own_sem.at[l, i])
                for i, (r, rows, c) in enumerate(weight_parts(l, wg, wu, wd))]

    def shared_load(l):
        return [pltpu.make_async_copy(src_of(r, c, l), shw.at[l, rows, :], sh_sem.at[l, i])
                for i, (r, rows, c) in enumerate(weight_parts(l, sg, su, sd))]

    def partner_load(l):
        return [rdma(src_of(r, c, l), wall.at[l, mine, rows, :], w_send.at[l, i], w_recv.at[l, i], dev_p)
                for i, (r, rows, c) in enumerate(weight_parts(l, wg, wu, wd))]

    tok_load = pltpu.make_async_copy(tok, tbuf.at[0, 0], tok_sem)
    tok_load.start()
    for c in own_load(0):
        c.start()

    barrier = pltpu.get_barrier_semaphore()
    for dev in (dev_l, dev_r, dev_o, dev_p):
        pl.semaphore_signal(barrier, inc=1, device_id={'ep': dev}, device_id_type=MESH)
    pl.semaphore_wait(barrier, 4)

    def ag_copies(l, c, src, kinds):
        lo, hi = pl.ds(c * ch, ch), pl.ds(half + c * ch, ch)
        form = [(lo, 1, lo, dev_r), (hi, 2, lo, dev_r), (hi, 1, hi, dev_l), (lo, 2, hi, dev_l)]
        return [rdma(src.at[form[k][0], :], tbuf.at[l, form[k][1], form[k][2], :],
                     ag_send.at[l, k, c], ag_recv.at[l, k, c], form[k][3]) for k in kinds]

    def ag_start(l, src, c_list, kinds):
        for c in c_list:
            for cp in ag_copies(l, c, src, kinds):
                cp.start()

    def relay(l, c, side):
        rows = pl.ds(c * ch, ch) if side == 0 else pl.ds(half + c * ch, ch)
        dev = dev_r if side == 0 else dev_l
        return rdma(tbuf.at[l, 1, rows, :], tbuf.at[l, 3, rows, :], rl_send.at[l, side, c], rl_recv.at[l, side, c], dev)

    ag_start(0, tok, range(CHUNKS), (0, 2))
    cl = lax.rem(chip + n_chip - 1, n_chip)
    cr = lax.rem(chip + 1, n_chip)
    co = lax.rem(chip + 2, n_chip)
    coefs = [rdma(coef.at[cr], crecv.at[0], c_send.at[0], c_recv.at[0], dev_r),
             rdma(coef.at[cl], crecv.at[1], c_send.at[1], c_recv.at[1], dev_l),
             rdma(coef.at[co], crecv.at[2], c_send.at[2], c_recv.at[2], dev_o)]
    for c in coefs:
        c.start()
    for c in partner_load(0):
        c.start()
    ag_start(0, tok, range(CHUNKS), (1, 3))
    for c in shared_load(0) + own_load(1):
        c.start()
    for c in partner_load(1):
        c.start()
    for c in shared_load(1):
        c.start()

    eye = lax.broadcasted_iota(jnp.int32, (half, half), 0) == lax.broadcasted_iota(jnp.int32, (half, half), 1)

    def column(row):
        return jnp.sum(jnp.where(eye, jnp.broadcast_to(row, (half, half)), 0.0), axis=1, keepdims=True)

    def gates(l, u, q):
        s = l * 4 + q
        lo, hi = pl.ds(0, half), pl.ds(half, half)
        if u == 0:
            a, b = coef[chip, s, :, lo], coef[chip, s, :, hi]
        elif u == 1:
            a, b = crecv[0, s, :, lo], crecv[1, s, :, hi]
        elif u == 2:
            a, b = crecv[0, s, :, hi], crecv[1, s, :, lo]
        else:
            a, b = crecv[2, s, :, lo], crecv[2, s, :, hi]
        return jnp.concatenate([column(a), column(b)], axis=0)

    def swiglu(x, w):
        g = jnp.dot(x, w[pl.ds(0, d_model), :], preferred_element_type=f32)
        u = jnp.dot(x, w[pl.ds(d_model, d_model), :], preferred_element_type=f32)
        inner = (jax.nn.silu(g) * u).astype(bf16)
        return [jnp.dot(inner, w[pl.ds(2 * d_model + j * d_ff, d_ff), :], preferred_element_type=f32) for j in range(2)]

    def unit(l, u):
        def one(q, carry):
            outs = swiglu(tbuf[l, u], wall.at[l, q])
            col = gates(l, u, q)
            for j in range(2):
                cols = pl.ds(j * d_ff, d_ff)
                pbuf[u, :, cols] = pbuf[u, :, cols] + col * outs[j]
            return carry

        if u == 0:
            x = tbuf[l, 0]
            outs = swiglu(x, shw.at[l])
            for j in range(2):
                pbuf[0, :, j * d_ff:(j + 1) * d_ff] = x[:, j * d_ff:(j + 1) * d_ff].astype(f32) + outs[j]
        else:
            pbuf[u] = jnp.zeros(pbuf.shape[1:], f32)
        lax.fori_loop(0, 4, one, 0)

    info = []
    for m in range(2 * LAYERS):
        s, t = tab[m], tab[4 + m]
        s_chip, s_loc = s >> 2, s & 3
        t_chip, t_loc = t >> 2, t & 3
        dist = [(t_chip - s_chip) & (n_chip - 1), (s_chip - t_chip) & (n_chip - 1)]
        info.append((m // 2, s_loc, s_chip == chip, dist, t_chip == chip, t_loc))

    def piece_row(i, d):
        if isinstance(i, int):
            ph, rest = i // per_phase, i % per_phase
        else:
            ph, rest = lax.div(i, per_phase), lax.rem(i, per_phase)
        return pl.multiple_of(ph * d_model + core * 2 * quarter + d * quarter + rest * PIECE, PIECE)

    def mod(k, n):
        return k % n if isinstance(k, int) else lax.rem(k, n)

    def move_copy(k, d):
        slot = mod(k, SEND_SLOTS)
        return rdma(msend.at[d, slot], mrecv.at[d, mod(k, RECV_SLOTS)], mv_send.at[d, slot], mv_recv.at[d, mod(k, RECV_SEMS)],
                    dev_r if d == 0 else dev_l)

    def out_copies(i, d):
        slot = mod(i, OUT_SLOTS)
        rows = pl.ds(piece_row(i, d), PIECE)
        own = pltpu.make_async_copy(mout.at[slot, d, 0], w_out.at[:, :, rows, :], mo_local.at[slot, d])
        far = rdma(mout.at[slot, d, 1], w_out.at[:, :, rows, :], mo_send.at[slot, d], mo_recv, dev_p)
        return own, far

    def pick(options, which):
        v = options[0]
        for q in range(1, 4):
            v = jnp.where(which == q, options[q], v)
        return v

    def emit(i, reuse):
        slot = mod(i, OUT_SLOTS)
        for d in range(2):
            if reuse:
                own, far = out_copies(i - OUT_SLOTS, d)
                own.wait()
                far.wait_send()
            rows = pl.ds(piece_row(i, d), PIECE)
            held = [[wall[l, q, rows, :] for q in range(4)] for l in range(LAYERS)]
            near = [[wall[l, base + j, rows, :] for j in range(2)] for l in range(LAYERS)]
            away = [[wall[l, 2 - base + j, rows, :] for j in range(2)] for l in range(LAYERS)]
            vals = []
            for m, (l, s_loc, _, dist, _, _) in enumerate(info):
                h = dist[d]
                v = pick(held[l], s_loc)
                for j in range(3):
                    v = jnp.where(h == j + 1, mrecv[d, mod(i + j * LAG, RECV_SLOTS), m], v)
                vals.append(v)
            for which in range(2):
                for j in range(2):
                    q = base + j if which == 0 else 2 - base + j
                    for l in range(LAYERS):
                        v = (away if which else near)[l][j]
                        for m in (2 * l, 2 * l + 1):
                            hit = jnp.logical_and(info[m][4], info[m][5] == q)
                            v = jnp.where(hit, vals[m], v)
                        mout[slot, d, which, l, j] = v
            own, far = out_copies(i, d)
            own.start()
            far.start()

    def step(k, has_own, has_in, reuse_send, emits, reuse_out):
        if has_in:
            for d in range(2):
                move_copy(k - LAG, d).wait_recv()
        if has_own or has_in == 1:
            slot = mod(k, SEND_SLOTS)
            for d in range(2):
                if reuse_send:
                    move_copy(k - SEND_SLOTS, d).wait_send()
                if has_own:
                    rows = pl.ds(piece_row(k, d), PIECE)
                    held = [[wall[l, q, rows, :] for q in range(4)] for l in range(LAYERS)]
                for m, (l, s_loc, is_src, _, _, _) in enumerate(info):
                    if has_own:
                        v = pick(held[l], s_loc)
                        if has_in:
                            v = jnp.where(is_src, v, mrecv[d, mod(k - LAG, RECV_SLOTS), m])
                    else:
                        v = mrecv[d, mod(k - LAG, RECV_SLOTS), m]
                    msend[d, slot, m] = v
                move_copy(k, d).start()
        if emits:
            emit(k - 3 * LAG, reuse_out)

    first_full = 3 * LAG + OUT_SLOTS

    def one_step(k):
        if k < n_step:
            step(k, k < n_piece, 1 if k >= LAG else 0, k >= SEND_SLOTS, k >= 3 * LAG, k >= first_full)
        else:
            step(k, False, 2, False, k >= 3 * LAG, k >= first_full)

    cursor = [0]

    def moves(count):
        a = cursor[0]
        b = min(a + count, n_step + LAG)
        cursor[0] = b
        k = a
        while k < b and k < first_full:
            one_step(k)
            k += 1
        mid = min(b, n_piece)
        if k < mid:
            def loop_body(kk, carry):
                step(kk, True, 1, True, True, True)
                return carry
            lax.fori_loop(k, mid, loop_body, 0)
            k = mid
        while k < b:
            one_step(k)
            k += 1

    for l in range(LAYERS):
        for c in range(CHUNKS):
            for cp in ag_copies(l, c, tbuf.at[l, 0], (0, 2)):
                cp.wait_recv()
            relay(l, c, 0).start()
            relay(l, c, 1).start()
        if l == 0:
            for c in own_load(0):
                c.wait()
            for c in partner_load(0):
                c.wait_recv()
            for c in coefs:
                c.wait_recv()
        lo, hi = pl.ds(0, half), pl.ds(half, half)

        def pure(ll):
            return [rdma(pbuf.at[1, lo, :], rpure.at[ll, lo, :], pu_send.at[ll, 0], pu_recv.at[ll, 0], dev_l),
                    rdma(pbuf.at[1, hi, :], rpure.at[ll, hi, :], pu_send.at[ll, 1], pu_recv.at[ll, 1], dev_r)]

        def opp(ll, c):
            a, b = pl.ds(c * ch, ch), pl.ds(half + c * ch, ch)
            return [rdma(pbuf.at[3, a, :], ropp.at[ll, b, :], op_send.at[ll, 0, c], op_recv.at[ll, 0, c], dev_r),
                    rdma(pbuf.at[3, b, :], ropp.at[ll, a, :], op_send.at[ll, 1, c], op_recv.at[ll, 1, c], dev_l)]

        def summed(ll, c):
            a, b = pl.ds(c * ch, ch), pl.ds(half + c * ch, ch)
            return [rdma(pbuf.at[2, a, :], rsum.at[ll, b, :], sm_send.at[ll, 0, c], sm_recv.at[ll, 0, c], dev_l),
                    rdma(pbuf.at[2, b, :], rsum.at[ll, a, :], sm_send.at[ll, 1, c], sm_recv.at[ll, 1, c], dev_r)]

        if l > 0:
            for cp in pure(l - 1):
                cp.wait_send()
        unit(l, 1)
        for cp in pure(l):
            cp.start()
        if l == 0:
            for c in own_load(1):
                c.wait()
            for c in partner_load(1):
                c.wait_recv()
        moves(PLACE['u1'][l])
        for c in range(CHUNKS):
            for cp in ag_copies(l, c, tbuf.at[l, 0], (1, 3)):
                cp.wait_recv()
            if l > 0:
                for cp in summed(l - 1, c):
                    cp.wait_send()
        unit(l, 2)
        moves(PLACE['u2'][l])
        for c in range(CHUNKS):
            relay(l, c, 0).wait_recv()
            relay(l, c, 1).wait_recv()
            if l > 0:
                for cp in opp(l - 1, c):
                    cp.wait_send()
        unit(l, 3)
        for c in range(CHUNKS):
            for cp in opp(l, c):
                cp.start()
        moves(PLACE['u3'][l])
        if l == 0:
            tok_load.wait()
        for c in shared_load(l):
            c.wait()
        unit(l, 0)
        moves(PLACE['own'][l])
        for c in range(CHUNKS):
            a, b = pl.ds(c * ch, ch), pl.ds(half + c * ch, ch)
            for cp in opp(l, c):
                cp.wait_recv()
            for rows in (a, b):
                pbuf[2, rows, :] = pbuf[2, rows, :] + ropp[l, rows, :]
            for cp in summed(l, c):
                cp.start()
            moves(PLACE['sum'][l])
        for cp in pure(l):
            cp.wait_recv()
        for c in range(CHUNKS):
            a, b = pl.ds(c * ch, ch), pl.ds(half + c * ch, ch)
            for cp in summed(l, c):
                cp.wait_recv()
            for rows in (a, b):
                new = (pbuf[0, rows, :] + rpure[l, rows, :] + rsum[l, rows, :]).astype(bf16)
                if l + 1 < LAYERS:
                    tbuf[l + 1, 0, rows, :] = new
                else:
                    tok_out[rows, :] = new
            if l + 1 < LAYERS:
                ag_start(l + 1, tbuf.at[l + 1, 0], [c], (0, 1, 2, 3))
            moves(PLACE['fin'][l])

    moves(n_step + LAG)

    for k in range(n_step - SEND_SLOTS, n_step):
        for d in range(2):
            move_copy(k, d).wait_send()
    for i in range(n_piece - OUT_SLOTS, n_piece):
        for d in range(2):
            own, far = out_copies(i, d)
            own.wait()
            far.wait_send()
    arrived = w_out.at[:, :, pl.ds(0, 6 * quarter), :]
    pltpu.make_async_copy(arrived, arrived, mo_recv).wait()
    last = LAYERS - 1
    for cp in pure(last):
        cp.wait_send()
    for c in range(CHUNKS):
        for cp in opp(last, c) + summed(last, c):
            cp.wait_send()
    for l in range(LAYERS):
        for c in range(CHUNKS):
            for cp in ag_copies(l, c, tok if l == 0 else tbuf.at[l, 0], (0, 1, 2, 3)):
                cp.wait_send()
            relay(l, c, 0).wait_send()
            relay(l, c, 1).wait_send()
        for cp in partner_load(l):
            cp.wait_send()
    for cp in coefs:
        cp.wait_send()


def fused(n_ep, tab, coef, tok, wg, wu, wd, sg, su, sd):
    toks, d_model = tok.shape
    d_ff = sg.shape[-1]
    n_chip = n_ep // 2
    rows = 3 * d_model
    f32, bf16 = jnp.float32, jnp.bfloat16
    any_spec = pl.BlockSpec(memory_space=pl.ANY)
    vmem = pl.BlockSpec(memory_space=pltpu.VMEM)
    dma = pltpu.SemaphoreType.DMA
    return pl.pallas_call(
        functools.partial(kernel, n_chip, (toks, d_model, d_ff)),
        out_shape=(jax.ShapeDtypeStruct((toks, d_model), bf16),
                   jax.ShapeDtypeStruct((LAYERS, 2, rows, d_ff), bf16)),
        in_specs=[pl.BlockSpec(memory_space=pltpu.SMEM), vmem] + [any_spec] * 7,
        out_specs=(vmem, any_spec),
        scratch_shapes=[
            pltpu.VMEM((LAYERS, 4, rows, d_ff), bf16),
            pltpu.VMEM((LAYERS, rows, d_ff), bf16),
            pltpu.VMEM((LAYERS, 4, toks, d_model), bf16),
            pltpu.VMEM((4, toks, d_model), f32),
            pltpu.VMEM((LAYERS, toks, d_model), f32),
            pltpu.VMEM((LAYERS, toks, d_model), f32),
            pltpu.VMEM((LAYERS, toks, d_model), f32),
            pltpu.VMEM((3,) + coef.shape[1:], f32),
            pltpu.VMEM((2, RECV_SLOTS, 4, PIECE, d_ff), bf16),
            pltpu.VMEM((2, SEND_SLOTS, 4, PIECE, d_ff), bf16),
            pltpu.VMEM((OUT_SLOTS, 2, 2, LAYERS, 2, PIECE, d_ff), bf16),
            dma((LAYERS, 4)), dma((LAYERS, 4)), dma((LAYERS, 4)), dma((LAYERS, 4)), dma(()), dma((3,)), dma((3,)),
            dma((LAYERS, 4, CHUNKS)), dma((LAYERS, 4, CHUNKS)), dma((LAYERS, 2, CHUNKS)), dma((LAYERS, 2, CHUNKS)),
            dma((LAYERS, 2)), dma((LAYERS, 2)),
            dma((LAYERS, 2, CHUNKS)), dma((LAYERS, 2, CHUNKS)), dma((LAYERS, 2, CHUNKS)), dma((LAYERS, 2, CHUNKS)),
            dma((2, SEND_SLOTS)), dma((2, RECV_SEMS)), dma((OUT_SLOTS, 2)), dma((OUT_SLOTS, 2)), dma(()),
        ],
        compiler_params=pltpu.CompilerParams(collective_id=0, has_side_effects=True, vmem_limit_bytes=67043328),
    )(tab, coef, tok, wg, wu, wd, sg, su, sd)


def solution(mesh):
    n_ep = mesh.shape['ep']

    def body(tok_in, routes, gate_vals, w_gate, w_up, w_down, sh_gate, sh_up, sh_down, old_map, move_slot, move_expert):
        n_slot = old_map.shape[1]
        slot_ids = jnp.arange(n_slot, dtype=jnp.int32)
        same = old_map[:, :, None] == old_map[:, None, :]
        serve = jnp.min(jnp.where(same, slot_ids[None, None, :], n_slot), axis=2) == slot_ids[None, :]
        served = jnp.where(serve, old_map, -1)
        hit = routes.transpose(0, 2, 1)[:, None] == served[:, :, None, None]
        coef = jnp.sum(jnp.where(hit, gate_vals.transpose(0, 2, 1)[:, None], 0.0), axis=2)
        coef = coef.reshape(LAYERS, n_slot // 4, 4, 1, -1).transpose(1, 0, 2, 3, 4)
        coef = coef.reshape(n_slot // 4, LAYERS * 4, 1, -1)
        holds = old_map[:, None, :] == move_expert[:, :, None]
        source = jnp.min(jnp.where(holds, slot_ids[None, None, :], n_slot), axis=2)
        tab = jnp.concatenate([source.reshape(-1), move_slot.reshape(-1)]).astype(jnp.int32)
        tok, packed = fused(n_ep, tab, coef, tok_in, w_gate, w_up, w_down, sh_gate, sh_up, sh_down)
        d_model, d_ff = w_gate.shape[2:]
        new_gate = packed[:, :, :d_model]
        new_up = packed[:, :, d_model:2 * d_model]
        new_down = jnp.concatenate([packed[:, :, 2 * d_model:2 * d_model + d_ff], packed[:, :, 2 * d_model + d_ff:]], axis=3)
        return (tok, new_gate, new_up, new_down)

    weight_spec = P(None, TOKEN_AXES, None, None)
    route_spec = P(None, TOKEN_AXES, None)
    map_spec = P(None, 'replica')
    shared_spec = P(None, None, None)
    tok_spec = P(TOKEN_AXES, None)
    return jax.shard_map(body, mesh=mesh, in_specs=(tok_spec, route_spec, route_spec, weight_spec, weight_spec, weight_spec, shared_spec, shared_spec, shared_spec, map_spec, map_spec, map_spec), out_specs=(tok_spec, weight_spec, weight_spec, weight_spec), check_vma=False)
```

time: 429 us -> 227 us (0.53)
  waiting for transfers between devices: 228 us -> 0 us
  Pallas kernels: 0 us -> 208 us
  matrix products: 71.3 us -> 0 us
  local copies, waits for them, and re-layouts: 60.2 us -> 10.7 us
  blocking collectives: 27.9 us -> 0 us
  other arithmetic: 26.9 us -> 6.6 us
  between operations: 14 us -> 0.68 us
    pallas_call x0 -> x1, Pallas kernels: none -> 208 us  [fused(): pl.pallas_call(functools.partial(kernel, n_chip, (toks, d_model, d_ff)),...]
    psum x1 -> x0, waiting for transfers between devices: 111 us -> none  [body(): arrived = lax.psum(outgoing, 'ep')]
    reduce_scatter x2 -> x0, waiting for transfers between devices: 77.4 us -> none  [moe_layer(): lax.psum_scatter(partial_sum, 'ep', scatter_dimension=0, tiled=True)]
    dot_general x8 -> x0, matrix products: 71.3 us -> none  [the longest x2 40.5 us: moe_layer(): jnp.einsum('jnf,jfd->jnd', inner_act, expert_w[2], preferred_element_type...]
    gather x12 -> x0, local copies, waits for them, and re-layouts: 40.5 us -> none  [the longest x6 20.3 us: send_moved(): jnp.take(weight_arr, local_idx, axis=0)]
    all_gather x2 -> x0, waiting for transfers between devices: 38 us -> none  [moe_layer(): gathered = lax.all_gather(hidden, 'ep', axis=0, tiled=True)]
    all_gather x2 -> x0, blocking collectives: 27.9 us -> none  [the longest x1 14.9 us: body(): gate_all = lax.all_gather(gate_vals, 'ep', axis=1, tiled=True)]
    another operation x7 -> x0, other arithmetic: 15.6 us -> none  [the longest x2 8.52 us: body(): new_gate = jnp.stack([placed[0][0], placed[1][0]])]
  transfers between devices with their start and end apart: 5 -> 0, of which waited for: 5 -> 0; matrix products, arithmetic and copies ran while one was open for 9% -> 0% of each run, Pallas kernels for 0% -> 0%
where the time goes in v1:
time: 227 us; the launch traced here: 226 us
  Pallas kernels  208 us (92%)
  local copies, waits for them, and re-layouts  10.7 us (5%)
  other arithmetic  6.6 us (3%)
    pallas_call x1, Pallas kernels, fused(): pl.pallas_call(functools.partial(kernel, n_chip, (toks, d_model, d_ff)),...  208 us
    slice x1, local copies, waits for them, and re-layouts, body(): new_up = packed[:, :, d_model:2 * d_model]  5.86 us

profile of v1, /device:TPU:81, one launch (start us, length us, event | category | flops | bytes accessed | tf_op | source)
XLA Modules:
  0.0 226.3 jit_solution(16868496700904858813)
XLA Ops:
  0.6 0.8 reshape.27
  1.4 0.9 fusion
  2.3 0.1 reshape.26
  2.4 0.6 pad_add_fusion.tab
  2.9 0.9 select_reduce_fusion.1
  3.9 0.7 compare_select_fusion.1
  4.6 0.9 select_reduce_fusion
  5.5 0.6 copy.18
  6.1 208.4 %shard_map.147 = (bf16[256,1024]{1,0:T(8,128)(2,1)}, bf16[2,2,3072,512]{3,2,1,0:T(8,128)(2,1)}) custom-call(s32[8]{0:T(128)} %pad_add_fusion.tab, f32[4,8,1,256]{3,2,1,0:T(1,128)} %bitcast.6, bf16[256,1024]{1,0:T(8,128)(2,1)} %tok.1, bf16[2,2,1024,512]{3,2,1,0:T(8,128)(2,1)} %wg.1, bf16[2,2,1024,512]{3,2,1,0:T(8,128)(2,1)} %wu.1, ...), custom_call_target="tpu_custom_call" | custom-call | tf_op jit(solution)/shard_map/pallas_call | solution.py:414
  214.5 5.9 %fusion.2 = (bf16[2,2,1024,512]{3,2,1,0:T(8,128)(2,1)}, bf16[2,2,1024,512]{3,2,1,0:T(8,128)(2,1)}) fusion(bf16[2,2,3072,512]{3,2,1,0:T(8,128)(2,1)} %get-tuple-element.7), kind=kLoop, calls=%fused_computation.8 | loop fusion | bytes 16777216 | tf_op jit(solution)/shard_map/slice | solution.py:461
  220.4 2.5 %fusion.1 = (bf16[2,2,512,512]{3,2,1,0:T(8,128)(2,1)S(1)}, bf16[2,2,512,512]{3,2,1,0:T(8,128)(2,1)S(1)}) fusion(bf16[2,2,3072,512]{3,2,1,0:T(8,128)(2,1)} %get-tuple-element.7), kind=kLoop, calls=%fused_computation.7 | loop fusion | bytes 8388608 | tf_op jit(solution)/shard_map/slice | solution.py:462
  222.9 0.0 copy-start
  222.9 2.6 %pad_maximum_fusion = bf16[2,2,512,1024]{3,2,1,0:T(8,128)(2,1)} fusion(bf16[2,2,512,512]{3,2,1,0:T(8,128)(2,1)S(1)} %get-tuple-element.9, bf16[2,2,512,512]{3,2,1,0:T(8,128)(2,1)S(1)} %get-tuple-element.8), kind=kLoop, calls=%fused_computation | loop fusion | flops 8388608 | bytes 8388608 | tf_op jit(solution)/shard_map/concatenate | solution.py:462
  225.6 0.0 copy-done
  225.6 0.8 copy.20
  (1 shorter events, 0.0 us)
Async XLA Ops:
  222.9 2.7 %copy-start = (bf16[256,1024]{1,0:T(8,128)(2,1)S(1)}, bf16[256,1024]{1,0:T(8,128)(2,1)}, u32[]{:S(2)}) copy-start(bf16[256,1024]{1,0:T(8,128)(2,1)} %get-tuple-element.16) | copy-start | bytes 1572868

commit v2 on v1

--- a/solution.py
+++ b/solution.py
@@ -11,18 +11,18 @@
 MESH = pl.DeviceIdType.MESH
 CHUNKS = 4
 PIECE = 16
-LAG = 2
-SEND_SLOTS = 4
+LAG = 4
+SEND_SLOTS = LAG + 2
 OUT_SLOTS = 4
-RECV_SEMS = 8
-RECV_SLOTS = 16
+RECV_SEMS = 4 * LAG
+RECV_SLOTS = 6 * LAG + 2
 LAYERS = 2
-PLACE = {'u1': (2, 2), 'u2': (2, 2), 'u3': (2, 2), 'own': (2, 2), 'sum': (1, 1), 'fin': (1, 1)}
-
-
-def kernel(n_chip, dims, tab, coef, tok, wg, wu, wd, sg, su, sd,
-           tok_out, w_out,
-           wall, shw, tbuf, pbuf, rpure, ropp, rsum, crecv, mrecv, msend, mout,
+PLACE = {'relay': (0, 0), 'u1': (0, 4), 'u2': (0, 4), 'u3': (2, 4), 'own': (4, 4), 'sum': (2, 2), 'fin': (2, 1)}
+
+
+def kernel(n_chip, dims, old_map, move_slot, move_expert, routes, gate_vals, tok, wg, wu, wd, sg, su, sd,
+           tok_out, og, ou, od,
+           wall, shw, tbuf, pbuf, rpure, ropp, rsum, coef, crecv, mrecv, msend, mout,
            own_sem, w_send, w_recv, sh_sem, tok_sem, c_send, c_recv,
            ag_send, ag_recv, rl_send, rl_recv, pu_send, pu_recv,
            op_send, op_recv, sm_send, sm_recv,
@@ -79,6 +79,16 @@
     for c in own_load(0):
         c.start()
 
+    n_slot = n_chip * 4
+    for l in range(LAYERS):
+        ids = [old_map[l, q] for q in range(n_slot)]
+        for q in range(n_slot):
+            want = ids[q]
+            for p in range(q):
+                want = jnp.where(ids[p] == ids[q], -1, want)
+            row = jnp.sum(jnp.where(routes[l] == want, gate_vals[l], 0.0), axis=0, keepdims=True)
+            coef[q // 4, l * 4 + q % 4] = row
+
     barrier = pltpu.get_barrier_semaphore()
     for dev in (dev_l, dev_r, dev_o, dev_p):
         pl.semaphore_signal(barrier, inc=1, device_id={'ep': dev}, device_id_type=MESH)
@@ -143,27 +153,12 @@
         inner = (jax.nn.silu(g) * u).astype(bf16)
         return [jnp.dot(inner, w[pl.ds(2 * d_model + j * d_ff, d_ff), :], preferred_element_type=f32) for j in range(2)]
 
-    def unit(l, u):
-        def one(q, carry):
-            outs = swiglu(tbuf[l, u], wall.at[l, q])
-            col = gates(l, u, q)
-            for j in range(2):
-                cols = pl.ds(j * d_ff, d_ff)
-                pbuf[u, :, cols] = pbuf[u, :, cols] + col * outs[j]
-            return carry
-
-        if u == 0:
-            x = tbuf[l, 0]
-            outs = swiglu(x, shw.at[l])
-            for j in range(2):
-                pbuf[0, :, j * d_ff:(j + 1) * d_ff] = x[:, j * d_ff:(j + 1) * d_ff].astype(f32) + outs[j]
-        else:
-            pbuf[u] = jnp.zeros(pbuf.shape[1:], f32)
-        lax.fori_loop(0, 4, one, 0)
-
     info = []
     for m in range(2 * LAYERS):
-        s, t = tab[m], tab[4 + m]
+        t, want = move_slot[m // 2, m % 2], move_expert[m // 2, m % 2]
+        s = jnp.int32(0)
+        for q in range(n_slot - 1, 0, -1):
+            s = jnp.where(old_map[m // 2, q] == want, q, s)
         s_chip, s_loc = s >> 2, s & 3
         t_chip, t_loc = t >> 2, t & 3
         dist = [(t_chip - s_chip) & (n_chip - 1), (s_chip - t_chip) & (n_chip - 1)]
@@ -184,11 +179,15 @@
         return rdma(msend.at[d, slot], mrecv.at[d, mod(k, RECV_SLOTS)], mv_send.at[d, slot], mv_recv.at[d, mod(k, RECV_SEMS)],
                     dev_r if d == 0 else dev_l)
 
-    def out_copies(i, d):
+    def out_copies(i, d, ph=0):
         slot = mod(i, OUT_SLOTS)
-        rows = pl.ds(piece_row(i, d), PIECE)
-        own = pltpu.make_async_copy(mout.at[slot, d, 0], w_out.at[:, :, rows, :], mo_local.at[slot, d])
-        far = rdma(mout.at[slot, d, 1], w_out.at[:, :, rows, :], mo_send.at[slot, d], mo_recv, dev_p)
+        row = d * quarter + mod(i, per_phase) * PIECE
+        if ph < 2:
+            dst = (og, ou)[ph].at[:, :, pl.ds(pl.multiple_of(row + core * 2 * quarter, PIECE), PIECE), :]
+        else:
+            dst = od.at[:, :, pl.ds(pl.multiple_of(row, PIECE), PIECE), pl.ds(pl.multiple_of(core * d_ff, d_ff), d_ff)]
+        own = pltpu.make_async_copy(mout.at[slot, d, 0], dst, mo_local.at[slot, d])
+        far = rdma(mout.at[slot, d, 1], dst, mo_send.at[slot, d], mo_recv.at[ph], dev_p)
         return own, far
 
     def pick(options, which):
@@ -197,7 +196,7 @@
             v = jnp.where(which == q, options[q], v)
         return v
 
-    def emit(i, reuse):
+    def emit(i, reuse, ph):
         slot = mod(i, OUT_SLOTS)
         for d in range(2):
             if reuse:
@@ -224,11 +223,11 @@
                             hit = jnp.logical_and(info[m][4], info[m][5] == q)
                             v = jnp.where(hit, vals[m], v)
                         mout[slot, d, which, l, j] = v
-            own, far = out_copies(i, d)
+            own, far = out_copies(i, d, ph)
             own.start()
             far.start()
 
-    def step(k, has_own, has_in, reuse_send, emits, reuse_out):
+    def step(k, has_own, has_in, reuse_send, emits, reuse_out, ph=None):
         if has_in:
             for d in range(2):
                 move_copy(k - LAG, d).wait_recv()
@@ -250,7 +249,7 @@
                     msend[d, slot, m] = v
                 move_copy(k, d).start()
         if emits:
-            emit(k - 3 * LAG, reuse_out)
+            emit(k - 3 * LAG, reuse_out, (k - 3 * LAG) // per_phase if ph is None else ph)
 
     first_full = 3 * LAG + OUT_SLOTS
 
@@ -270,23 +269,66 @@
         while k < b and k < first_full:
             one_step(k)
             k += 1
-        mid = min(b, n_piece)
-        if k < mid:
-            def loop_body(kk, carry):
-                step(kk, True, 1, True, True, True)
+        while k < min(b, n_piece):
+            ph = (k - 3 * LAG) // per_phase
+            mid = min(b, n_piece, 3 * LAG + (ph + 1) * per_phase)
+
+            def loop_body(kk, carry, ph=ph):
+                step(kk, True, 1, True, True, True, ph)
                 return carry
+
             lax.fori_loop(k, mid, loop_body, 0)
             k = mid
         while k < b:
             one_step(k)
             k += 1
 
+    def unit(l, u, per_slot=0):
+        def one(q):
+            outs = swiglu(tbuf[l, u], wall.at[l, q])
+            col = gates(l, u, q)
+            for j in range(2):
+                cols = pl.ds(j * d_ff, d_ff)
+                pbuf[u, :, cols] = pbuf[u, :, cols] + col * outs[j]
+
+        if u == 0:
+            x = tbuf[l, 0]
+            outs = swiglu(x, shw.at[l])
+            for j in range(2):
+                pbuf[0, :, j * d_ff:(j + 1) * d_ff] = x[:, j * d_ff:(j + 1) * d_ff].astype(f32) + outs[j]
+        else:
+            pbuf[u] = jnp.zeros(pbuf.shape[1:], f32)
+        first = cursor[0]
+        end = first + 4 * per_slot
+        ph = (first - 3 * LAG) // per_phase
+        if per_slot and first_full <= first and end <= min(n_piece, 3 * LAG + (ph + 1) * per_phase):
+            cursor[0] = end
+
+            def body(q, carry):
+                one(q)
+                for r in range(per_slot):
+                    step(first + q * per_slot + r, True, 1, True, True, True, ph)
+                return carry
+
+            lax.fori_loop(0, 4, body, 0)
+        elif per_slot:
+            for q in range(4):
+                one(q)
+                moves(per_slot)
+        else:
+            def plain(q, carry):
+                one(q)
+                return carry
+
+            lax.fori_loop(0, 4, plain, 0)
+
     for l in range(LAYERS):
         for c in range(CHUNKS):
             for cp in ag_copies(l, c, tbuf.at[l, 0], (0, 2)):
                 cp.wait_recv()
             relay(l, c, 0).start()
             relay(l, c, 1).start()
+            moves(PLACE['relay'][l])
         if l == 0:
             for c in own_load(0):
                 c.wait()
@@ -314,6 +356,7 @@
             for cp in pure(l - 1):
                 cp.wait_send()
         unit(l, 1)
+        moves(PLACE['u1'][l])
         for cp in pure(l):
             cp.start()
         if l == 0:
@@ -321,7 +364,6 @@
                 c.wait()
             for c in partner_load(1):
                 c.wait_recv()
-        moves(PLACE['u1'][l])
         for c in range(CHUNKS):
             for cp in ag_copies(l, c, tbuf.at[l, 0], (1, 3)):
                 cp.wait_recv()
@@ -382,8 +424,9 @@
             own, far = out_copies(i, d)
             own.wait()
             far.wait_send()
-    arrived = w_out.at[:, :, pl.ds(0, 6 * quarter), :]
-    pltpu.make_async_copy(arrived, arrived, mo_recv).wait()
+    for ph in range(3):
+        arrived = (og, ou)[ph].at[:, :, pl.ds(0, 2 * quarter), :] if ph < 2 else od.at[:, :, :, pl.ds(0, d_ff)]
+        pltpu.make_async_copy(arrived, arrived, mo_recv.at[ph]).wait()
     last = LAYERS - 1
     for cp in pure(last):
         cp.wait_send()
@@ -402,7 +445,7 @@
         cp.wait_send()
 
 
-def fused(n_ep, tab, coef, tok, wg, wu, wd, sg, su, sd):
+def fused(n_ep, old_map, move_slot, move_expert, routes, gate_vals, tok, wg, wu, wd, sg, su, sd):
     toks, d_model = tok.shape
     d_ff = sg.shape[-1]
     n_chip = n_ep // 2
@@ -410,13 +453,13 @@
     f32, bf16 = jnp.float32, jnp.bfloat16
     any_spec = pl.BlockSpec(memory_space=pl.ANY)
     vmem = pl.BlockSpec(memory_space=pltpu.VMEM)
+    smem = pl.BlockSpec(memory_space=pltpu.SMEM)
     dma = pltpu.SemaphoreType.DMA
     return pl.pallas_call(
         functools.partial(kernel, n_chip, (toks, d_model, d_ff)),
-        out_shape=(jax.ShapeDtypeStruct((toks, d_model), bf16),
-                   jax.ShapeDtypeStruct((LAYERS, 2, rows, d_ff), bf16)),
-        in_specs=[pl.BlockSpec(memory_space=pltpu.SMEM), vmem] + [any_spec] * 7,
-        out_specs=(vmem, any_spec),
+        out_shape=(jax.ShapeDtypeStruct((toks, d_model), bf16),) + tuple(jax.ShapeDtypeStruct(w.shape, bf16) for w in (wg, wu, wd)),
+        in_specs=[smem] * 3 + [vmem] * 2 + [any_spec] * 7,
+        out_specs=(vmem, any_spec, any_spec, any_spec),
         scratch_shapes=[
             pltpu.VMEM((LAYERS, 4, rows, d_ff), bf16),
             pltpu.VMEM((LAYERS, rows, d_ff), bf16),
@@ -425,7 +468,8 @@
             pltpu.VMEM((LAYERS, toks, d_model), f32),
             pltpu.VMEM((LAYERS, toks, d_model), f32),
             pltpu.VMEM((LAYERS, toks, d_model), f32),
-            pltpu.VMEM((3,) + coef.shape[1:], f32),
+            pltpu.VMEM((n_chip, LAYERS * 4, 1, toks), f32),
+            pltpu.VMEM((3, LAYERS * 4, 1, toks), f32),
             pltpu.VMEM((2, RECV_SLOTS, 4, PIECE, d_ff), bf16),
             pltpu.VMEM((2, SEND_SLOTS, 4, PIECE, d_ff), bf16),
             pltpu.VMEM((OUT_SLOTS, 2, 2, LAYERS, 2, PIECE, d_ff), bf16),
@@ -433,34 +477,18 @@
             dma((LAYERS, 4, CHUNKS)), dma((LAYERS, 4, CHUNKS)), dma((LAYERS, 2, CHUNKS)), dma((LAYERS, 2, CHUNKS)),
             dma((LAYERS, 2)), dma((LAYERS, 2)),
             dma((LAYERS, 2, CHUNKS)), dma((LAYERS, 2, CHUNKS)), dma((LAYERS, 2, CHUNKS)), dma((LAYERS, 2, CHUNKS)),
-            dma((2, SEND_SLOTS)), dma((2, RECV_SEMS)), dma((OUT_SLOTS, 2)), dma((OUT_SLOTS, 2)), dma(()),
+            dma((2, SEND_SLOTS)), dma((2, RECV_SEMS)), dma((OUT_SLOTS, 2)), dma((OUT_SLOTS, 2)), dma((3,)),
         ],
         compiler_params=pltpu.CompilerParams(collective_id=0, has_side_effects=True, vmem_limit_bytes=67043328),
-    )(tab, coef, tok, wg, wu, wd, sg, su, sd)
+    )(old_map, move_slot, move_expert, routes, gate_vals, tok, wg, wu, wd, sg, su, sd)
 
 
 def solution(mesh):
     n_ep = mesh.shape['ep']
 
     def body(tok_in, routes, gate_vals, w_gate, w_up, w_down, sh_gate, sh_up, sh_down, old_map, move_slot, move_expert):
-        n_slot = old_map.shape[1]
-        slot_ids = jnp.arange(n_slot, dtype=jnp.int32)
-        same = old_map[:, :, None] == old_map[:, None, :]
-        serve = jnp.min(jnp.where(same, slot_ids[None, None, :], n_slot), axis=2) == slot_ids[None, :]
-        served = jnp.where(serve, old_map, -1)
-        hit = routes.transpose(0, 2, 1)[:, None] == served[:, :, None, None]
-        coef = jnp.sum(jnp.where(hit, gate_vals.transpose(0, 2, 1)[:, None], 0.0), axis=2)
-        coef = coef.reshape(LAYERS, n_slot // 4, 4, 1, -1).transpose(1, 0, 2, 3, 4)
-        coef = coef.reshape(n_slot // 4, LAYERS * 4, 1, -1)
-        holds = old_map[:, None, :] == move_expert[:, :, None]
-        source = jnp.min(jnp.where(holds, slot_ids[None, None, :], n_slot), axis=2)
-        tab = jnp.concatenate([source.reshape(-1), move_slot.reshape(-1)]).astype(jnp.int32)
-        tok, packed = fused(n_ep, tab, coef, tok_in, w_gate, w_up, w_down, sh_gate, sh_up, sh_down)
-        d_model, d_ff = w_gate.shape[2:]
-        new_gate = packed[:, :, :d_model]
-        new_up = packed[:, :, d_model:2 * d_model]
-        new_down = jnp.concatenate([packed[:, :, 2 * d_model:2 * d_model + d_ff], packed[:, :, 2 * d_model + d_ff:]], axis=3)
-        return (tok, new_gate, new_up, new_down)
+        return fused(n_ep, old_map, move_slot, move_expert, routes.transpose(0, 2, 1), gate_vals.transpose(0, 2, 1),
+                     tok_in, w_gate, w_up, w_down, sh_gate, sh_up, sh_down)
 
     weight_spec = P(None, TOKEN_AXES, None, None)
     route_spec = P(None, TOKEN_AXES, None)

time: 227 us -> 205 us (0.903)
  Pallas kernels: 208 us -> 192 us
  other arithmetic: 6.6 us -> 0 us
    pallas_call x1, Pallas kernels: 208 us -> 192 us  [fused(): pl.pallas_call(functools.partial(kernel, n_chip, (toks, d_model, d_ff)),...]
    unnamed x3 -> x8, local copies, waits for them, and re-layouts: 0.8 us -> 12.2 us
    slice x2 -> x0, local copies, waits for them, and re-layouts: 8.35 us -> none  [the longest x1 5.86 us: body(): new_up = packed[:, :, d_model:2 * d_model]]
    concatenate x2 -> x0, other arithmetic: 3.23 us -> none  [the longest x1 2.64 us: body(): jnp.concatenate([packed[:, :, 2 * d_model:2 * d_model + d_ff], packed[:,...]
where the time goes in v2:
time: 205 us; the launch traced here: 204 us
  Pallas kernels  192 us (94%)
  local copies, waits for them, and re-layouts  12.2 us (6%)
    pallas_call x1, Pallas kernels, fused(): pl.pallas_call(functools.partial(kernel, n_chip, (toks, d_model, d_ff)),...  192 us
    unnamed x8, local copies, waits for them, and re-layouts  12.2 us

profile of v2, /device:TPU:81, one launch (start us, length us, event | category | flops | bytes accessed | tf_op | source)
XLA Modules:
  0.0 204.4 jit_solution(16714632532676210822)
XLA Ops:
  0.6 191.5 %shard_map.147 = (bf16[256,1024]{1,0:T(8,128)(2,1)}, bf16[2,2,1024,512]{3,2,1,0:T(8,128)(2,1)}, bf16[2,2,1024,512]{3,2,1,0:T(8,128)(2,1)}, bf16[2,2,512,1024]{3,2,1,0:T(8,128)(2,1)}) custom-call(s32[2,16]{1,0:T(2,128)} %old_map.1, s32[2,2]{1,0:T(2,128)} %move_slot.1, s32[2,2]{1,0:T(2,128)} %move_expert.1, s32[2,8,256]{2,1,0:T(8,128)} %bitcast.2, ...), custom_call_target="tpu_custom_call" | custom-call | tf_op jit(solution)/shard_map/pallas_call | solution.py:458
  192.2 1.9 copy.20
  194.1 0.0 copy-start.1
  194.1 4.6 %copy.21 = bf16[2,2,1024,512]{3,2,1,0:T(8,128)(2,1)} copy(bf16[2,2,1024,512]{3,2,1,0:T(8,128)(2,1)} %get-tuple-element.9) | data formatting | bytes 8388608
  198.7 0.0 copy-done.1
  198.7 0.0 copy-start
  198.7 2.1 %copy.22 = bf16[2,2,1024,512]{3,2,1,0:T(8,128)(2,1)} copy(bf16[2,2,1024,512]{3,2,1,0:T(8,128)(2,1)S(1)} %copy-done.1) | data formatting | bytes 8388608
  200.8 1.6 copy-done
  202.4 2.0 copy.23
Async XLA Ops:
  194.1 4.6 %copy-start.1 = (bf16[2,2,1024,512]{3,2,1,0:T(8,128)(2,1)S(1)}, bf16[2,2,1024,512]{3,2,1,0:T(8,128)(2,1)}, u32[]{:S(2)}) copy-start(bf16[2,2,1024,512]{3,2,1,0:T(8,128)(2,1)} %get-tuple-element.10) | copy-start | bytes 12582916
  198.7 3.7 %copy-start = (bf16[2,2,512,1024]{3,2,1,0:T(8,128)(2,1)S(1)}, bf16[2,2,512,1024]{3,2,1,0:T(8,128)(2,1)}, u32[]{:S(2)}) copy-start(bf16[2,2,512,1024]{3,2,1,0:T(8,128)(2,1)} %get-tuple-element.11) | copy-start | bytes 12582916

commit v3 on v2

--- a/solution.py
+++ b/solution.py
@@ -17,6 +17,7 @@
 RECV_SEMS = 4 * LAG
 RECV_SLOTS = 6 * LAG + 2
 LAYERS = 2
+VMEM_LIMIT = 46 * 2 ** 20
 PLACE = {'relay': (0, 0), 'u1': (0, 4), 'u2': (0, 4), 'u3': (2, 4), 'own': (4, 4), 'sum': (2, 2), 'fin': (2, 1)}
 
 
@@ -26,7 +27,7 @@
            own_sem, w_send, w_recv, sh_sem, tok_sem, c_send, c_recv,
            ag_send, ag_recv, rl_send, rl_recv, pu_send, pu_recv,
            op_send, op_recv, sm_send, sm_recv,
-           mv_send, mv_recv, mo_local, mo_send, mo_recv):
+           mv_send, mv_recv, mo_send, mo_recv):
     toks, d_model, d_ff = dims
     half = toks // 2
     ch = half // CHUNKS
@@ -67,7 +68,7 @@
                 for i, (r, rows, c) in enumerate(weight_parts(l, wg, wu, wd))]
 
     def shared_load(l):
-        return [pltpu.make_async_copy(src_of(r, c, l), shw.at[l, rows, :], sh_sem.at[l, i])
+        return [pltpu.make_async_copy(src_of(r, c, l), shw.at[rows, :], sh_sem.at[l, i])
                 for i, (r, rows, c) in enumerate(weight_parts(l, sg, su, sd))]
 
     def partner_load(l):
@@ -126,8 +127,6 @@
         c.start()
     for c in partner_load(1):
         c.start()
-    for c in shared_load(1):
-        c.start()
 
     eye = lax.broadcasted_iota(jnp.int32, (half, half), 0) == lax.broadcasted_iota(jnp.int32, (half, half), 1)
 
@@ -179,16 +178,16 @@
         return rdma(msend.at[d, slot], mrecv.at[d, mod(k, RECV_SLOTS)], mv_send.at[d, slot], mv_recv.at[d, mod(k, RECV_SEMS)],
                     dev_r if d == 0 else dev_l)
 
-    def out_copies(i, d, ph=0):
+    def place(ph, rest, d):
+        row = pl.multiple_of(d * quarter + rest * PIECE, PIECE)
+        if ph < 2:
+            return (og, ou)[ph], pl.ds(pl.multiple_of(row + core * 2 * quarter, PIECE), PIECE), pl.ds(0, d_ff)
+        return od, pl.ds(row, PIECE), pl.ds(pl.multiple_of(core * d_ff, d_ff), d_ff)
+
+    def far_copy(i, d, ph=0):
         slot = mod(i, OUT_SLOTS)
-        row = d * quarter + mod(i, per_phase) * PIECE
-        if ph < 2:
-            dst = (og, ou)[ph].at[:, :, pl.ds(pl.multiple_of(row + core * 2 * quarter, PIECE), PIECE), :]
-        else:
-            dst = od.at[:, :, pl.ds(pl.multiple_of(row, PIECE), PIECE), pl.ds(pl.multiple_of(core * d_ff, d_ff), d_ff)]
-        own = pltpu.make_async_copy(mout.at[slot, d, 0], dst, mo_local.at[slot, d])
-        far = rdma(mout.at[slot, d, 1], dst, mo_send.at[slot, d], mo_recv.at[ph], dev_p)
-        return own, far
+        ref, rows, cols = place(ph, mod(i, per_phase), d)
+        return rdma(mout.at[slot, d], ref.at[:, :, rows, cols], mo_send.at[slot, d], mo_recv.at[ph], dev_p)
 
     def pick(options, which):
         v = options[0]
@@ -200,9 +199,7 @@
         slot = mod(i, OUT_SLOTS)
         for d in range(2):
             if reuse:
-                own, far = out_copies(i - OUT_SLOTS, d)
-                own.wait()
-                far.wait_send()
+                far_copy(i - OUT_SLOTS, d).wait_send()
             rows = pl.ds(piece_row(i, d), PIECE)
             held = [[wall[l, q, rows, :] for q in range(4)] for l in range(LAYERS)]
             near = [[wall[l, base + j, rows, :] for j in range(2)] for l in range(LAYERS)]
@@ -222,10 +219,12 @@
                         for m in (2 * l, 2 * l + 1):
                             hit = jnp.logical_and(info[m][4], info[m][5] == q)
                             v = jnp.where(hit, vals[m], v)
-                        mout[slot, d, which, l, j] = v
-            own, far = out_copies(i, d, ph)
-            own.start()
-            far.start()
+                        if which:
+                            mout[slot, d, l, j] = v
+                        else:
+                            ref, to_rows, to_cols = place(ph, mod(i, per_phase), d)
+                            ref[l, j, to_rows, to_cols] = v
+            far_copy(i, d, ph).start()
 
     def step(k, has_own, has_in, reuse_send, emits, reuse_out, ph=None):
         if has_in:
@@ -293,7 +292,7 @@
 
         if u == 0:
             x = tbuf[l, 0]
-            outs = swiglu(x, shw.at[l])
+            outs = swiglu(x, shw)
             for j in range(2):
                 pbuf[0, :, j * d_ff:(j + 1) * d_ff] = x[:, j * d_ff:(j + 1) * d_ff].astype(f32) + outs[j]
         else:
@@ -339,18 +338,18 @@
         lo, hi = pl.ds(0, half), pl.ds(half, half)
 
         def pure(ll):
-            return [rdma(pbuf.at[1, lo, :], rpure.at[ll, lo, :], pu_send.at[ll, 0], pu_recv.at[ll, 0], dev_l),
-                    rdma(pbuf.at[1, hi, :], rpure.at[ll, hi, :], pu_send.at[ll, 1], pu_recv.at[ll, 1], dev_r)]
+            return [rdma(pbuf.at[1, lo, :], rpure.at[lo, :], pu_send.at[ll, 0], pu_recv.at[ll, 0], dev_l),
+                    rdma(pbuf.at[1, hi, :], rpure.at[hi, :], pu_send.at[ll, 1], pu_recv.at[ll, 1], dev_r)]
 
         def opp(ll, c):
             a, b = pl.ds(c * ch, ch), pl.ds(half + c * ch, ch)
-            return [rdma(pbuf.at[3, a, :], ropp.at[ll, b, :], op_send.at[ll, 0, c], op_recv.at[ll, 0, c], dev_r),
-                    rdma(pbuf.at[3, b, :], ropp.at[ll, a, :], op_send.at[ll, 1, c], op_recv.at[ll, 1, c], dev_l)]
+            return [rdma(pbuf.at[3, a, :], ropp.at[b, :], op_send.at[ll, 0, c], op_recv.at[ll, 0, c], dev_r),
+                    rdma(pbuf.at[3, b, :], ropp.at[a, :], op_send.at[ll, 1, c], op_recv.at[ll, 1, c], dev_l)]
 
         def summed(ll, c):
             a, b = pl.ds(c * ch, ch), pl.ds(half + c * ch, ch)
-            return [rdma(pbuf.at[2, a, :], rsum.at[ll, b, :], sm_send.at[ll, 0, c], sm_recv.at[ll, 0, c], dev_l),
-                    rdma(pbuf.at[2, b, :], rsum.at[ll, a, :], sm_send.at[ll, 1, c], sm_recv.at[ll, 1, c], dev_r)]
+            return [rdma(pbuf.at[2, a, :], rsum.at[b, :], sm_send.at[ll, 0, c], sm_recv.at[ll, 0, c], dev_l),
+                    rdma(pbuf.at[2, b, :], rsum.at[a, :], sm_send.at[ll, 1, c], sm_recv.at[ll, 1, c], dev_r)]
 
         if l > 0:
             for cp in pure(l - 1):
@@ -388,13 +387,16 @@
         for c in shared_load(l):
             c.wait()
         unit(l, 0)
+        if l + 1 < LAYERS:
+            for c in shared_load(l + 1):
+                c.start()
         moves(PLACE['own'][l])
         for c in range(CHUNKS):
             a, b = pl.ds(c * ch, ch), pl.ds(half + c * ch, ch)
             for cp in opp(l, c):
                 cp.wait_recv()
             for rows in (a, b):
-                pbuf[2, rows, :] = pbuf[2, rows, :] + ropp[l, rows, :]
+                pbuf[2, rows, :] = pbuf[2, rows, :] + ropp[rows, :]
             for cp in summed(l, c):
                 cp.start()
             moves(PLACE['sum'][l])
@@ -405,7 +407,7 @@
             for cp in summed(l, c):
                 cp.wait_recv()
             for rows in (a, b):
-                new = (pbuf[0, rows, :] + rpure[l, rows, :] + rsum[l, rows, :]).astype(bf16)
+                new = (pbuf[0, rows, :] + rpure[rows, :] + rsum[rows, :]).astype(bf16)
                 if l + 1 < LAYERS:
                     tbuf[l + 1, 0, rows, :] = new
                 else:
@@ -421,9 +423,7 @@
             move_copy(k, d).wait_send()
     for i in range(n_piece - OUT_SLOTS, n_piece):
         for d in range(2):
-            own, far = out_copies(i, d)
-            own.wait()
-            far.wait_send()
+            far_copy(i, d).wait_send()
     for ph in range(3):
         arrived = (og, ou)[ph].at[:, :, pl.ds(0, 2 * quarter), :] if ph < 2 else od.at[:, :, :, pl.ds(0, d_ff)]
         pltpu.make_async_copy(arrived, arrived, mo_recv.at[ph]).wait()
@@ -451,35 +451,35 @@
     n_chip = n_ep // 2
     rows = 3 * d_model
     f32, bf16 = jnp.float32, jnp.bfloat16
-    any_spec = pl.BlockSpec(memory_space=pl.ANY)
+    hbm = pl.BlockSpec(memory_space=pltpu.HBM)
     vmem = pl.BlockSpec(memory_space=pltpu.VMEM)
     smem = pl.BlockSpec(memory_space=pltpu.SMEM)
     dma = pltpu.SemaphoreType.DMA
     return pl.pallas_call(
         functools.partial(kernel, n_chip, (toks, d_model, d_ff)),
-        out_shape=(jax.ShapeDtypeStruct((toks, d_model), bf16),) + tuple(jax.ShapeDtypeStruct(w.shape, bf16) for w in (wg, wu, wd)),
-        in_specs=[smem] * 3 + [vmem] * 2 + [any_spec] * 7,
-        out_specs=(vmem, any_spec, any_spec, any_spec),
+        out_shape=(jax.ShapeDtypeStruct((toks, d_model), bf16),) + tuple(pltpu.VMEM(w.shape, bf16) for w in (wg, wu, wd)),
+        in_specs=[smem] * 3 + [vmem] * 2 + [hbm] * 7,
+        out_specs=(vmem, vmem, vmem, vmem),
         scratch_shapes=[
             pltpu.VMEM((LAYERS, 4, rows, d_ff), bf16),
-            pltpu.VMEM((LAYERS, rows, d_ff), bf16),
+            pltpu.VMEM((rows, d_ff), bf16),
             pltpu.VMEM((LAYERS, 4, toks, d_model), bf16),
             pltpu.VMEM((4, toks, d_model), f32),
-            pltpu.VMEM((LAYERS, toks, d_model), f32),
-            pltpu.VMEM((LAYERS, toks, d_model), f32),
-            pltpu.VMEM((LAYERS, toks, d_model), f32),
+            pltpu.VMEM((toks, d_model), f32),
+            pltpu.VMEM((toks, d_model), f32),
+            pltpu.VMEM((toks, d_model), f32),
             pltpu.VMEM((n_chip, LAYERS * 4, 1, toks), f32),
             pltpu.VMEM((3, LAYERS * 4, 1, toks), f32),
             pltpu.VMEM((2, RECV_SLOTS, 4, PIECE, d_ff), bf16),
             pltpu.VMEM((2, SEND_SLOTS, 4, PIECE, d_ff), bf16),
-            pltpu.VMEM((OUT_SLOTS, 2, 2, LAYERS, 2, PIECE, d_ff), bf16),
+            pltpu.VMEM((OUT_SLOTS, 2, LAYERS, 2, PIECE, d_ff), bf16),
             dma((LAYERS, 4)), dma((LAYERS, 4)), dma((LAYERS, 4)), dma((LAYERS, 4)), dma(()), dma((3,)), dma((3,)),
             dma((LAYERS, 4, CHUNKS)), dma((LAYERS, 4, CHUNKS)), dma((LAYERS, 2, CHUNKS)), dma((LAYERS, 2, CHUNKS)),
             dma((LAYERS, 2)), dma((LAYERS, 2)),
             dma((LAYERS, 2, CHUNKS)), dma((LAYERS, 2, CHUNKS)), dma((LAYERS, 2, CHUNKS)), dma((LAYERS, 2, CHUNKS)),
-            dma((2, SEND_SLOTS)), dma((2, RECV_SEMS)), dma((OUT_SLOTS, 2)), dma((OUT_SLOTS, 2)), dma((3,)),
+            dma((2, SEND_SLOTS)), dma((2, RECV_SEMS)), dma((OUT_SLOTS, 2)), dma((3,)),
         ],
-        compiler_params=pltpu.CompilerParams(collective_id=0, has_side_effects=True, vmem_limit_bytes=67043328),
+        compiler_params=pltpu.CompilerParams(collective_id=0, has_side_effects=True, vmem_limit_bytes=VMEM_LIMIT),
     )(old_map, move_slot, move_expert, routes, gate_vals, tok, wg, wu, wd, sg, su, sd)
 
 

time: 205 us -> 199 us (0.971)
  local copies, waits for them, and re-layouts: 12.2 us -> 6.84 us
    unnamed x8 -> x6, local copies, waits for them, and re-layouts: 12.2 us -> 6.84 us
where the time goes in v3:
time: 199 us
  Pallas kernels  191 us (96%)
  local copies, waits for them, and re-layouts  6.84 us (3%)
    pallas_call x1, Pallas kernels, fused(): pl.pallas_call(functools.partial(kernel, n_chip, (toks, d_model, d_ff)),...  191 us
    unnamed x6, local copies, waits for them, and re-layouts  6.84 us

profile of v3, /device:TPU:81, one launch (start us, length us, event | category | flops | bytes accessed | tf_op | source)
XLA Modules:
  0.0 199.0 jit_solution(437644121991734074)
XLA Ops:
  0.6 191.5 %shard_map.147 = (bf16[256,1024]{1,0:T(8,128)(2,1)}, bf16[2,2,1024,512]{3,2,1,0:T(8,128)(2,1)S(1)}, bf16[2,2,1024,512]{3,2,1,0:T(8,128)(2,1)S(1)}, bf16[2,2,512,1024]{3,2,1,0:T(8,128)(2,1)S(1)}) custom-call(s32[2,16]{1,0:T(2,128)} %old_map.1, s32[2,2]{1,0:T(2,128)} %move_slot.1, s32[2,2]{1,0:T(2,128)} %move_expert.1, s32[2,8,256]{2,1,0:T(8,128)} %bitcast.2, ...), custom_call_target="tpu_custom_call" | custom-call | tf_op jit(solution)/shard_map/pallas_call | solution.py:458
  192.1 2.0 %copy.20 = bf16[2,2,1024,512]{3,2,1,0:T(8,128)(2,1)} copy(bf16[2,2,1024,512]{3,2,1,0:T(8,128)(2,1)S(1)} %get-tuple-element.5) | data formatting | bytes 8388608
  194.1 2.0 %copy.21 = bf16[2,2,1024,512]{3,2,1,0:T(8,128)(2,1)} copy(bf16[2,2,1024,512]{3,2,1,0:T(8,128)(2,1)S(1)} %get-tuple-element.6) | data formatting | bytes 8388608
  196.1 0.0 copy-start
  196.1 2.0 %copy.22 = bf16[2,2,512,1024]{3,2,1,0:T(8,128)(2,1)} copy(bf16[2,2,512,1024]{3,2,1,0:T(8,128)(2,1)S(1)} %get-tuple-element.7) | data formatting | bytes 8388608
  198.2 0.0 copy-done
  198.2 0.8 copy.23
Async XLA Ops:
  196.1 2.0 %copy-start = (bf16[256,1024]{1,0:T(8,128)(2,1)S(1)}, bf16[256,1024]{1,0:T(8,128)(2,1)}, u32[]{:S(2)}) copy-start(bf16[256,1024]{1,0:T(8,128)(2,1)} %get-tuple-element.12) | copy-start | bytes 1572868

commit v4 on v3

--- a/solution.py
+++ b/solution.py
@@ -457,7 +457,7 @@
     dma = pltpu.SemaphoreType.DMA
     return pl.pallas_call(
         functools.partial(kernel, n_chip, (toks, d_model, d_ff)),
-        out_shape=(jax.ShapeDtypeStruct((toks, d_model), bf16),) + tuple(pltpu.VMEM(w.shape, bf16) for w in (wg, wu, wd)),
+        out_shape=(pltpu.VMEM((toks, d_model), bf16),) + tuple(pltpu.VMEM(w.shape, bf16) for w in (wg, wu, wd)),
         in_specs=[smem] * 3 + [vmem] * 2 + [hbm] * 7,
         out_specs=(vmem, vmem, vmem, vmem),
         scratch_shapes=[

time: 199 us -> 198 us (level)
    unnamed x6 -> x4, local copies, waits for them, and re-layouts: 6.84 us -> 6.83 us
where the time goes in v4:
time: 198 us
  Pallas kernels  191 us (96%)
  local copies, waits for them, and re-layouts  6.83 us (3%)
    pallas_call x1, Pallas kernels, fused(): pl.pallas_call(functools.partial(kernel, n_chip, (toks, d_model, d_ff)),...  191 us
    unnamed x4, local copies, waits for them, and re-layouts  6.83 us

profile of v4, /device:TPU:81, one launch (start us, length us, event | category | flops | bytes accessed | tf_op | source)
XLA Modules:
  0.0 198.2 jit_solution(974399053797919797)
XLA Ops:
  0.6 190.7 %shard_map.147 = (bf16[256,1024]{1,0:T(8,128)(2,1)S(1)}, bf16[2,2,1024,512]{3,2,1,0:T(8,128)(2,1)S(1)}, bf16[2,2,1024,512]{3,2,1,0:T(8,128)(2,1)S(1)}, bf16[2,2,512,1024]{3,2,1,0:T(8,128)(2,1)S(1)}) custom-call(s32[2,16]{1,0:T(2,128)} %old_map.1, s32[2,2]{1,0:T(2,128)} %move_slot.1, s32[2,2]{1,0:T(2,128)} %move_expert.1, s32[2,8,256]{2,1,0:T(8,128)} %bitcast.2, ...), custom_call_target="tpu_custom_call" | custom-call | tf_op jit(solution)/shard_map/pallas_call | solution.py:458
  191.3 0.8 copy.20
  192.1 2.0 %copy.21 = bf16[2,2,1024,512]{3,2,1,0:T(8,128)(2,1)} copy(bf16[2,2,1024,512]{3,2,1,0:T(8,128)(2,1)S(1)} %get-tuple-element.5) | data formatting | bytes 8388608
  194.1 2.0 %copy.22 = bf16[2,2,1024,512]{3,2,1,0:T(8,128)(2,1)} copy(bf16[2,2,1024,512]{3,2,1,0:T(8,128)(2,1)S(1)} %get-tuple-element.6) | data formatting | bytes 8388608
  196.2 2.0 %copy.23 = bf16[2,2,512,1024]{3,2,1,0:T(8,128)(2,1)} copy(bf16[2,2,512,1024]{3,2,1,0:T(8,128)(2,1)S(1)} %get-tuple-element.7) | data formatting | bytes 8388608
